TPU v7x, 32 devices: a whole 2x2x4 slice. The times are simulated.
32 devices in a mesh: row: 4 (over z), col: 8 (over y, x, core).
Axes of the slice: x: 2, y: 2, z: 4, core: 2. Of those that a mesh axis runs over, the one named last changes fastest.
Arguments:
- neighbor: int32 [32, 3072, 3072], P(None, 'col', 'row'), may hold values from 0 to 1, as said below
- true_coords: float32 [32, 3, 3072], P(None, None, ('row', 'col')), as said below
- pred_coords: float32 [32, 3, 3072], P(None, None, ('row', 'col')), as said below
- residue_mask: int32 [32, 3072], P(None, ('row', 'col')), may hold values from 0 to 1, as said below
- single: bfloat16 [32, 3072, 384], P(None, ('row', 'col'))
- ln_gain: float32 [384], replicated, may hold values from 0.1 to 1.9
- w_hidden: bfloat16 [384, 128], replicated, may hold values from -0.3125 to 0.3125
- b_hidden: float32 [128], replicated, may hold values from -3 to 3
- w_mid: bfloat16 [128, 128], replicated, may hold values from -0.5 to 0.5
- b_mid: float32 [128], replicated, may hold values from -3 to 3
- w_logits: bfloat16 [128, 50], replicated, may hold values from -1.5 to 1.5
- b_logits: float32 [50], replicated, may hold values from -4 to 4
Outputs:
- lddt_score: float32 [32, 3072], P(None, ('row', 'col'))
- residue_loss: float32 [32, 3072], P(None, ('row', 'col'))
- total_loss: float32 [], replicated
Inputs may be any that keep to these rules, and one draw needn't show every extreme that they name: `neighbor`: 0 or 1; 0 where j == i; 1 wherever 0 < |i - j| <= 8. `residue_mask`: per structure, 1 on a leading run of 1536 or more residues and 0 after it. `true_coords`: positions in angstroms. `pred_coords`: positions in angstroms.
All inputs are finite; a program needn't handle non-finite values.
Results may differ from a plain program's by a relative error of at most 0.00098.
Values sent between devices are 32-bit elements; how exact they have to be, the bound alone decides.
A program may use at most 128 MiB of HBM per device.

v0:
```python
import jax
import jax.numpy as jnp
from jax import lax
from jax.sharding import PartitionSpec as P

L = 3072
THRESHOLDS = (0.5, 1.0, 2.0, 4.0)


def from_root(shard, axis, root):
    mine = lax.axis_index(axis) == root
    return lax.psum(jnp.where(mine, shard, jnp.zeros_like(shard)), axis)


def tile_dist(rows_block, cols_block):
    total = (cols_block[:, 0, :, None] - rows_block[:, 0, None, :]) ** 2
    total = total + (cols_block[:, 1, :, None] - rows_block[:, 1, None, :]) ** 2
    total = total + (cols_block[:, 2, :, None] - rows_block[:, 2, None, :]) ** 2
    return jnp.sqrt(total + 1e-10)


def head_loss(lddt_value, single, ln_gain, w_hidden, b_hidden, w_mid, b_mid, w_logits, b_logits):
    features = single.astype(jnp.float32)
    average = jnp.mean(features, axis=-1, keepdims=True)
    centred = features - average
    variance = jnp.mean(centred * centred, axis=-1, keepdims=True)
    normed = (centred * lax.rsqrt(variance + 1e-05) * ln_gain).astype(jnp.bfloat16)
    first_hidden = jax.nn.relu(
        jnp.dot(normed, w_hidden, preferred_element_type=jnp.float32) + b_hidden
    ).astype(jnp.bfloat16)
    second_hidden = jax.nn.relu(
        jnp.dot(first_hidden, w_mid, preferred_element_type=jnp.float32) + b_mid
    ).astype(jnp.bfloat16)
    logits = jnp.dot(second_hidden, w_logits, preferred_element_type=jnp.float32) + b_logits
    log_total = jnp.log(jnp.sum(jnp.exp(logits), axis=-1))
    bins = logits.shape[-1]
    centers = (jnp.arange(bins).astype(jnp.float32) + 0.5) / bins
    closeness = jnp.exp(-((lddt_value[..., None] - centers) ** 2) * (bins * bins * 0.5))
    target = closeness / jnp.sum(closeness, axis=-1, keepdims=True)
    return log_total - jnp.sum(target * logits, axis=-1)


def local(
    neighbor,
    true_coords,
    pred_coords,
    residue_mask,
    single,
    ln_gain,
    w_hidden,
    b_hidden,
    w_mid,
    b_mid,
    w_logits,
    b_logits,
):
    valid = residue_mask.astype(jnp.float32)
    own_len = residue_mask.shape[1]
    stacked = jnp.concatenate([true_coords, pred_coords, valid[:, None, :]], axis=1)
    row_count = lax.axis_size("row")
    col_count = lax.axis_size("col")
    rows_len = L // row_count
    cols_len = L // col_count
    col_index = lax.axis_index("col")
    rows_part = lax.all_gather(stacked, "col", axis=2, tiled=True)
    offset = col_index * cols_len % rows_len
    column_piece = lax.dynamic_slice_in_dim(rows_part, offset, cols_len, 2)
    source_row = col_index * cols_len // rows_len
    cols_part = from_root(column_piece, "row", source_row)
    true_dist = tile_dist(rows_part[:, 0:3], cols_part[:, 0:3])
    pred_dist = tile_dist(rows_part[:, 3:6], cols_part[:, 3:6])
    mismatch = jnp.abs(pred_dist - true_dist)
    scores = jnp.zeros_like(mismatch)
    for threshold in THRESHOLDS:
        scores = scores + jax.nn.sigmoid(4.0 * (threshold - mismatch))
    scores = 0.25 * scores
    weights = neighbor.astype(jnp.float32) * rows_part[:, 6, None, :] * cols_part[:, 6, :, None]
    preserved = jnp.sum(weights * scores, axis=1)
    neighbors = jnp.sum(weights, axis=1)
    preserved_all, neighbors_all = lax.psum((preserved, neighbors), "col")
    preserved_own = lax.dynamic_slice_in_dim(preserved_all, col_index * own_len, own_len, 1)
    neighbors_own = lax.dynamic_slice_in_dim(neighbors_all, col_index * own_len, own_len, 1)
    lddt_score = preserved_own / jnp.maximum(neighbors_own, 1.0)
    residue_loss = valid * head_loss(
        lddt_score, single, ln_gain, w_hidden, b_hidden, w_mid, b_mid, w_logits, b_logits
    )
    loss_sum, valid_sum = lax.psum((jnp.sum(residue_loss), jnp.sum(valid)), ("row", "col"))
    total_loss = loss_sum / valid_sum
    return (lddt_score, residue_loss, total_loss)


def solution(mesh):
    placed = (
        P(None, "col", "row"),
        P(None, None, ("row", "col")),
        P(None, None, ("row", "col")),
        P(None, ("row", "col")),
        P(None, ("row", "col"), None),
        P(),
        P(),
        P(),
        P(),
        P(),
        P(),
        P(),
    )
    return jax.shard_map(
        local,
        mesh=mesh,
        in_specs=placed,
        out_specs=(P(None, ("row", "col")), P(None, ("row", "col")), P()),
        check_vma=False,
    )
```

profile of v0, /device:TPU:0, one launch (start us, length us, event | category | flops | bytes accessed | tf_op | source)
XLA Modules:
  0.0 312.7 jit_solution(15335422747212448188)
XLA Ops:
  7.3 0.7 convert_bitcast_fusion
  8.0 0.8 pad_maximum_fusion
  8.8 0.9 copy.33
  9.7 21.3 %all_gather.3 = f32[32,7,768]{0,1,2:T(8,128)S(1)} all-gather(f32[32,7,96]{0,1,2:T(8,128)} %copy.33), channel_id=1, replica_groups=mesh['row'=4,'col'=8] {'col'}, dimensions={2}, use_global_device_ids=true | all-gather | bytes 774144 | tf_op jit(solution)/shard_map/all_gather | solution.py:65
  31.0 1.3 dynamic-slice_select_fusion
  32.4 3.3 %fusion.31 = (f32[32,1,768]{0,1,2:T(1,128)}, f32[32,1,768]{0,1,2:T(1,128)}, f32[32,1,768]{0,1,2:T(1,128)}, f32[32,1,768]{0,1,2:T(1,128)}, f32[32,1,768]{0,1,2:T(...) fusion(f32[32,7,768]{0,1,2:T(8,128)S(1)} %all_gather.3), kind=kLoop, calls=%fused_computation.43 | loop fusion | bytes 1376256 | tf_op jit(solution)/shard_map/slice | solution.py:77
  35.6 2.3 convert_reduce_fusion
  37.9 2.8 fusion.4
  40.8 3.2 %maximum_convert_fusion = bf16[32,96,128]{2,1,0:T(8,128)(2,1)S(1)} fusion(bf16[32,96,384]{2,1,0:T(8,128)(2,1)} %param.16, f32[384]{0:T(512)} %param.17, f32[32,96]{1,0:T(8,128)S(1)} %add_rsqrt_fusion, f32[32,96]{1,0:T(8,128)S(1)} %broadcast_multiply_fusion, f32[128]{0:T(128)} %param.21, f32[128]{0:T(128)} %param.19, bf16[384,128]{1,0:T(8,128)(2,1)S(1)} %copy-done, ...), kind=kOutput, calls=%fused_computation.15 | convolution fusion | flops 410910720 | bytes 3303936 | tf_op jit(solution)/shard_map/dot_general | solution.py:32
  44.0 1.1 copy.34
  45.1 1.1 copy.37
  46.2 1.1 copy.39
  47.4 1.1 copy.41
  48.5 1.1 copy.43
  49.7 1.1 copy.45
  50.8 1.1 copy.47
  51.9 1.4 exponential_reduce_fusion
  53.4 48.4 %all-reduce.5.cloned.1.call-done = f32[32,7,384]{0,1,2:T(8,128)} async-done(((f32[32,7,384]{0,1,2:T(8,128)}), f32[32,7,384]{0,1,2:T(8,128)}) %all-reduce.5.cloned.1.call-update) | async-done | bytes 344080 | tf_op jit(solution)/shard_map/psum | solution.py:12
  101.7 6.8 %fusion.32 = (f32[32,1,384]{0,1,2:T(1,128)S(1)}, f32[32,1,384]{0,1,2:T(1,128)S(1)}, f32[32,1,384]{0,1,2:T(1,128)S(1)}, f32[32,1,384]{0,1,2:T(1,128)S(1)}, f32[32...) fusion(f32[32,7,384]{0,1,2:T(8,128)} %all-reduce.5.cloned.1.call-done), kind=kLoop, calls=%fused_computation.44 | loop fusion | bytes 688128 | tf_op jit(solution)/shard_map/slice | solution.py:77
  109.3 98.8 %multiply_reduce_fusion = (f32[32,768]{1,0:T(8,128)}, f32[32,768]{1,0:T(8,128)}) fusion(s32[32,384,768]{2,1,0:T(8,128)} %param.12, f32[32,768]{1,0:T(8,128)S(1)} %copy.47, f32[32,384]{1,0:T(8,128)S(1)} %copy.46, f32[32,768]{1,0:T(8,128)S(1)} %copy.45, f32[32,384]{1,0:T(8,128)S(1)} %copy.44, f32[32,768]{1,0:T(8,128)S(1)} %copy.43, f32[32,384]{1,0:T(8,128)S(1)} %copy.42, ...), kind=kLoop, calls=%fused_computation.1 | loop fusion | flops 471810048 | bytes 38977536 | tf_op jit(solution)/shard_map/reduce_sum | solution.py:78
  208.2 53.1 %all-reduce.7.cloned.1.call-done = (f32[32,768]{1,0:T(8,128)}, f32[32,768]{1,0:T(8,128)}) async-done(((f32[32,768]{1,0:T(8,128)}, f32[32,768]{1,0:T(8,128)}), (f32[32,768]{1,0:T(8,128)}, f32[32,768]{1,0:T(8,128)})) %all-reduce.7.cloned.1.call-update) | async-done | bytes 196624 | tf_op jit(solution)/shard_map/psum | solution.py:80
  261.3 0.9 maximum_divide_fusion
  262.6 1.3 fusion.30
  263.9 39.6 %all-reduce = (f32[]{:T(128)}, f32[]{:T(128)}) all-reduce(f32[]{:T(128)} %get-tuple-element.12, f32[]{:T(128)} %get-tuple-element.28), channel_id=1, replica_groups=mesh['row'=4,'col'=8] {'row','col'}, use_global_device_ids=true, to_apply=%region_11.12 | all-reduce | flops 2 | bytes 16 | tf_op jit(solution)/shard_map/psum | solution.py:87
  (21 shorter events, 1.3 us)
Async XLA Ops:
  7.2 33.6 %copy-start = (bf16[384,128]{1,0:T(8,128)(2,1)S(1)}, bf16[384,128]{1,0:T(8,128)(2,1)}, u32[]{:S(2)}) copy-start(bf16[384,128]{1,0:T(8,128)(2,1)} %param.18) | copy-start | bytes 294916
  7.2 94.6 %all-reduce.5.cloned.1.call-start = ((), (), s32[]{:S(2)}) async-start(), calls=%async_computation | async-start | bytes 3145728 | tf_op jit(solution)/shard_map/psum | solution.py:12
  32.3 228.9 %all-reduce.7.cloned.1.call-start = ((), (), s32[]{:S(2)}) async-start(), calls=%async_computation.1 | async-start | bytes 393216 | tf_op jit(solution)/shard_map/psum | solution.py:80
  109.3 153.3 %copy-start.1 = (s32[32,96]{1,0:T(8,128)S(1)}, s32[32,96]{1,0:T(8,128)}, u32[]{:S(2)}) copy-start(s32[32,96]{1,0:T(8,128)} %param.15) | copy-start | bytes 36868
  262.1 42.6 %copy-start.2 = (f32[32,96]{1,0:T(8,128)}, f32[32,96]{1,0:T(8,128)S(1)}, u32[]{:S(2)}) copy-start(f32[32,96]{1,0:T(8,128)S(1)} %maximum_divide_fusion) | copy-start | bytes 36868
Sparse Core Ops, SparseCore 0:
  32.5 69.2 all-reduce.4
  208.3 52.9 all-reduce.6
where the time goes:
time: 314 us; the launch traced here: 313 us
  other arithmetic  109 us (35%)
  waiting for transfers between devices  102 us (32%)
  blocking collectives  60.8 us (19%)
  local copies, waits for them, and re-layouts  19.7 us (6%)
  between operations  16.6 us (5%)
  matrix products  4.59 us (1%)
    reduce_sum x1, other arithmetic, local(): preserved = jnp.sum(weights * scores, axis=1)  98.8 us
    psum x1, waiting for transfers between devices, local(): preserved_all, neighbors_all = lax.psum((preserved, neighbors), 'col')  53.1 us
    psum x1, waiting for transfers between devices, from_root(): return lax.psum(jnp.where(mine, shard, jnp.zeros_like(shard)), axis)  48.4 us
    psum x1, blocking collectives, local(): lax.psum((jnp.sum(residue_loss), jnp.sum(valid)), ('row', 'col'))  39.6 us
    all_gather x1, blocking collectives, local(): rows_part = lax.all_gather(stacked, 'col', axis=2, tiled=True)  21.3 us
    slice x1, local copies, waits for them, and re-layouts, local(): cols_part[:, 6, :, None]  6.78 us
  transfers between devices with their start and end apart: 2, of which 2 were waited for; matrix products, arithmetic and copies ran while one was open for 7% of the time, Pallas kernels for 0%

commit v1 on v0

--- a/solution.py
+++ b/solution.py
@@ -2,6 +2,7 @@
 import jax.numpy as jnp
 from jax import lax
 from jax.sharding import PartitionSpec as P
+from jax.lax import axis_index, ppermute, psum
 
 L = 3072
 THRESHOLDS = (0.5, 1.0, 2.0, 4.0)
@@ -62,7 +63,19 @@
     rows_len = L // row_count
     cols_len = L // col_count
     col_index = lax.axis_index("col")
-    rows_part = lax.all_gather(stacked, "col", axis=2, tiled=True)
+    n_peers_all = psum(1, "col")
+    by_rank = [stacked]
+    for idx in range(n_peers_all - 1):
+        by_rank.append(
+            ppermute(
+                by_rank[-1],
+                "col",
+                [(dev_j, (dev_j + 1) % n_peers_all) for dev_j in range(n_peers_all)],
+            )
+        )
+    rows_part = jnp.roll(
+        jnp.concatenate(by_rank[::-1], axis=2), (axis_index("col") + 1) * stacked.shape[2], axis=2
+    )
     offset = col_index * cols_len % rows_len
     column_piece = lax.dynamic_slice_in_dim(rows_part, offset, cols_len, 2)
     source_row = col_index * cols_len // rows_len

time: 314 us -> 291 us (0.927)
  blocking collectives: 60.8 us -> 39.6 us
  local copies, waits for them, and re-layouts: 19.7 us -> 2.06 us
  waiting for transfers between devices: 102 us -> 118 us
    ppermute x0 -> x7, waiting for transfers between devices: none -> 27.7 us  [local(): ppermute(by_rank[-1], 'col', [(dev_j, (dev_j + 1) % n_peers_all) for dev_...]
    all_gather x1 -> x0, blocking collectives: 21.3 us -> none  [local(): rows_part = lax.all_gather(stacked, 'col', axis=2, tiled=True)]
    psum x1, waiting for transfers between devices: 48.4 us -> 36 us  [from_root(): return lax.psum(jnp.where(mine, shard, jnp.zeros_like(shard)), axis)]
    slice x2 -> x0, local copies, waits for them, and re-layouts: 10 us -> none  [the longest x1 6.78 us: local(): cols_part[:, 6, :, None]]
    sub x12 -> x0, local copies, waits for them, and re-layouts: 7.5 us -> none  [the longest x4 2.5 us: tile_dist(): total = total + (cols_block[:, 1, :, None] - rows_block[:, 1, None, :]) ** 2]
  transfers between devices with their start and end apart: 2 -> 9, of which waited for: 2 -> 9; matrix products, arithmetic and copies ran while one was open for 7% -> 3% of each run, Pallas kernels for 0% -> 0%
where the time goes in v1:
time: 291 us; the launch traced here: 290 us
  waiting for transfers between devices  118 us (41%)
  other arithmetic  109 us (37%)
  blocking collectives  39.6 us (14%)
  between operations  16.6 us (6%)
  matrix products  4.58 us (2%)
    reduce_sum x1, other arithmetic, local(): preserved = jnp.sum(weights * scores, axis=1)  98.8 us
    psum x1, waiting for transfers between devices, local(): preserved_all, neighbors_all = lax.psum((preserved, neighbors), 'col')  53.8 us
    psum x1, blocking collectives, local(): lax.psum((jnp.sum(residue_loss), jnp.sum(valid)), ('row', 'col'))  39.6 us
    psum x1, waiting for transfers between devices, from_root(): return lax.psum(jnp.where(mine, shard, jnp.zeros_like(shard)), axis)  36 us
    ppermute x7, waiting for transfers between devices, local(): ppermute(by_rank[-1], 'col', [(dev_j, (dev_j + 1) % n_peers_all) for dev_...  27.7 us
  transfers between devices with their start and end apart: 9, of which 9 were waited for; matrix products, arithmetic and copies ran while one was open for 3% of the time, Pallas kernels for 0%

profile of v1, /device:TPU:0, one launch (start us, length us, event | category | flops | bytes accessed | tf_op | source)
XLA Modules:
  0.0 289.9 jit_solution(3583000818786891710)
XLA Ops:
  7.2 0.7 convert_bitcast_fusion
  7.9 0.8 pad_maximum_fusion
  8.8 0.5 collective-permute-start
  9.3 5.3 %collective-permute-done = f32[32,7,96]{2,0,1:T(8,128)S(1)} collective-permute-done((f32[32,7,96]{2,0,1:T(8,128)S(1)}, f32[32,7,96]{2,0,1:T(8,128)S(1)}, u32[]{:S(2)}, u32[]{:S(2)}) %collective-permute-start) | collective-permute-done | bytes 86048 | tf_op jit(solution)/shard_map/ppermute | solution.py:70
  14.7 5.1 %collective-permute-done.1 = f32[32,7,96]{2,0,1:T(8,128)S(1)} collective-permute-done((f32[32,7,96]{2,0,1:T(8,128)S(1)}, f32[32,7,96]{2,0,1:T(8,128)S(1)}, u32[]{:S(2)}, u32[]{:S(2)}) %collective-permute-start.1) | collective-permute-done | bytes 86048 | tf_op jit(solution)/shard_map/ppermute | solution.py:70
  19.8 2.3 convert_reduce_fusion
  22.1 2.8 collective-permute-done.2
  24.9 5.1 %collective-permute-done.3 = f32[32,7,96]{2,0,1:T(8,128)S(1)} collective-permute-done((f32[32,7,96]{2,0,1:T(8,128)S(1)}, f32[32,7,96]{2,0,1:T(8,128)S(1)}, u32[]{:S(2)}, u32[]{:S(2)}) %collective-permute-start.3) | collective-permute-done | bytes 86048 | tf_op jit(solution)/shard_map/ppermute | solution.py:70
  30.0 2.8 fusion.4
  32.8 2.3 collective-permute-done.4
  35.2 5.1 %collective-permute-done.5 = f32[32,7,96]{2,0,1:T(8,128)S(1)} collective-permute-done((f32[32,7,96]{2,0,1:T(8,128)S(1)}, f32[32,7,96]{2,0,1:T(8,128)S(1)}, u32[]{:S(2)}, u32[]{:S(2)}) %collective-permute-start.5) | collective-permute-done | bytes 86048 | tf_op jit(solution)/shard_map/ppermute | solution.py:70
  40.3 3.2 %maximum_convert_fusion = bf16[32,96,128]{2,1,0:T(8,128)(2,1)S(1)} fusion(bf16[32,96,384]{2,1,0:T(8,128)(2,1)} %param.16, f32[384]{0:T(512)} %param.17, f32[32,96]{1,0:T(8,128)S(1)} %add_rsqrt_fusion, f32[32,96]{1,0:T(8,128)S(1)} %broadcast_multiply_fusion, f32[128]{0:T(128)} %param.21, f32[128]{0:T(128)} %param.19, bf16[384,128]{1,0:T(8,128)(2,1)S(1)} %copy-done, ...), kind=kOutput, calls=%fused_computation.15 | convolution fusion | flops 410910720 | bytes 3303936 | tf_op jit(solution)/shard_map/dot_general | solution.py:33
  43.5 1.9 collective-permute-done.6
  45.4 0.8 concatenate.10
  46.2 0.9 dynamic-slice_select_fusion
  47.2 1.4 exponential_reduce_fusion
  48.9 36.0 %all-reduce.5.cloned.1.call-done = f32[32,7,384]{2,0,1:T(8,128)} async-done(((f32[32,7,384]{2,0,1:T(8,128)}), f32[32,7,384]{2,0,1:T(8,128)}) %all-reduce.5.cloned.1.call-update) | async-done | bytes 344080 | tf_op jit(solution)/shard_map/psum | solution.py:13
  84.9 1.0 slice_bitcast_fusion.6
  85.9 98.8 %multiply_reduce_fusion = (f32[32,768]{1,0:T(8,128)}, f32[32,768]{1,0:T(8,128)}) fusion(s32[32,384,768]{2,1,0:T(8,128)} %param.12, f32[32,768]{1,0:T(8,128)S(1)} %get-tuple-element.17, f32[32,384]{1,0:T(8,128)S(1)} %get-tuple-element.19, f32[32,768]{1,0:T(8,128)S(1)} %get-tuple-element.12, f32[32,384]{1,0:T(8,128)S(1)} %get-tuple-element.20, ...), kind=kLoop, calls=%fused_computation.1 | loop fusion | flops 471810048 | bytes 38977536 | tf_op jit(solution)/shard_map/reduce_sum | solution.py:91
  184.8 53.8 %all-reduce.7.cloned.1.call-done = (f32[32,768]{1,0:T(8,128)}, f32[32,768]{1,0:T(8,128)}) async-done(((f32[32,768]{1,0:T(8,128)}, f32[32,768]{1,0:T(8,128)}), (f32[32,768]{1,0:T(8,128)}, f32[32,768]{1,0:T(8,128)})) %all-reduce.7.cloned.1.call-update) | async-done | bytes 196624 | tf_op jit(solution)/shard_map/psum | solution.py:93
  238.5 0.9 maximum_divide_fusion
  239.4 0.4 fusion.31
  239.9 1.3 fusion.30
  241.2 39.6 %all-reduce = (f32[]{:T(128)}, f32[]{:T(128)}) all-reduce(f32[]{:T(128)} %get-tuple-element.9, f32[]{:T(128)} %get-tuple-element.25), channel_id=1, replica_groups=mesh['row'=4,'col'=8] {'row','col'}, use_global_device_ids=true, to_apply=%region_11.12 | all-reduce | flops 2 | bytes 16 | tf_op jit(solution)/shard_map/psum | solution.py:100
  (20 shorter events, 0.4 us)
Async XLA Ops:
  7.2 33.1 %copy-start = (bf16[384,128]{1,0:T(8,128)(2,1)S(1)}, bf16[384,128]{1,0:T(8,128)(2,1)}, u32[]{:S(2)}) copy-start(bf16[384,128]{1,0:T(8,128)(2,1)} %param.18) | copy-start | bytes 294916
  7.2 77.7 %all-reduce.5.cloned.1.call-start = ((), (), s32[]{:S(2)}) async-start(), calls=%async_computation | async-start | bytes 688128 | tf_op jit(solution)/shard_map/psum | solution.py:13
  8.8 5.9 %collective-permute-start = (f32[32,7,96]{2,0,1:T(8,128)S(1)}, f32[32,7,96]{2,0,1:T(8,128)S(1)}, u32[]{:S(2)}, u32[]{:S(2)}) collective-permute-start(f32[32,7,96]{2,0,1:T(8,128)S(1)} %pad_maximum_fusion), channel_id=1, source_target_pairs={{0,1},{1,2},{2,3},{3,4},{4,5},{5,6},{6,7},{7,0},{8,9},{9,10},{10,1... | collective-permute-start | bytes 258056 | tf_op jit(solution)/shard_map/ppermute | solution.py:70
  14.7 5.1 %collective-permute-start.1 = (f32[32,7,96]{2,0,1:T(8,128)S(1)}, f32[32,7,96]{2,0,1:T(8,128)S(1)}, u32[]{:S(2)}, u32[]{:S(2)}) collective-permute-start(f32[32,7,96]{2,0,1:T(8,128)S(1)} %collective-permute-done), channel_id=1, source_target_pairs={{0,1},{1,2},{2,3},{3,4},{4,5},{5,6},{6,7},{7,0},{8,9},{9,10},{10,1... | collective-permute-start | bytes 258056 | tf_op jit(solution)/shard_map/ppermute | solution.py:70
  19.8 5.1 %collective-permute-start.2 = (f32[32,7,96]{2,0,1:T(8,128)S(1)}, f32[32,7,96]{2,0,1:T(8,128)S(1)}, u32[]{:S(2)}, u32[]{:S(2)}) collective-permute-start(f32[32,7,96]{2,0,1:T(8,128)S(1)} %collective-permute-done.1), channel_id=1, source_target_pairs={{0,1},{1,2},{2,3},{3,4},{4,5},{5,6},{6,7},{7,0},{8,9},{9,10},{10,1... | collective-permute-start | bytes 258056 | tf_op jit(solution)/shard_map/ppermute | solution.py:70
  24.9 5.1 %collective-permute-start.3 = (f32[32,7,96]{2,0,1:T(8,128)S(1)}, f32[32,7,96]{2,0,1:T(8,128)S(1)}, u32[]{:S(2)}, u32[]{:S(2)}) collective-permute-start(f32[32,7,96]{2,0,1:T(8,128)S(1)} %collective-permute-done.2), channel_id=1, source_target_pairs={{0,1},{1,2},{2,3},{3,4},{4,5},{5,6},{6,7},{7,0},{8,9},{9,10},{10,1... | collective-permute-start | bytes 258056 | tf_op jit(solution)/shard_map/ppermute | solution.py:70
  30.0 5.1 %collective-permute-start.4 = (f32[32,7,96]{2,0,1:T(8,128)S(1)}, f32[32,7,96]{2,0,1:T(8,128)S(1)}, u32[]{:S(2)}, u32[]{:S(2)}) collective-permute-start(f32[32,7,96]{2,0,1:T(8,128)S(1)} %collective-permute-done.3), channel_id=1, source_target_pairs={{0,1},{1,2},{2,3},{3,4},{4,5},{5,6},{6,7},{7,0},{8,9},{9,10},{10,1... | collective-permute-start | bytes 258056 | tf_op jit(solution)/shard_map/ppermute | solution.py:70
  35.1 5.1 %collective-permute-start.5 = (f32[32,7,96]{2,0,1:T(8,128)S(1)}, f32[32,7,96]{2,0,1:T(8,128)S(1)}, u32[]{:S(2)}, u32[]{:S(2)}) collective-permute-start(f32[32,7,96]{2,0,1:T(8,128)S(1)} %collective-permute-done.4), channel_id=1, source_target_pairs={{0,1},{1,2},{2,3},{3,4},{4,5},{5,6},{6,7},{7,0},{8,9},{9,10},{10,1... | collective-permute-start | bytes 258056 | tf_op jit(solution)/shard_map/ppermute | solution.py:70
  40.3 5.1 %collective-permute-start.6 = (f32[32,7,96]{2,0,1:T(8,128)S(1)}, f32[32,7,96]{2,0,1:T(8,128)S(1)}, u32[]{:S(2)}, u32[]{:S(2)}) collective-permute-start(f32[32,7,96]{2,0,1:T(8,128)S(1)} %collective-permute-done.5), channel_id=1, source_target_pairs={{0,1},{1,2},{2,3},{3,4},{4,5},{5,6},{6,7},{7,0},{8,9},{9,10},{10,1... | collective-permute-start | bytes 258056 | tf_op jit(solution)/shard_map/ppermute | solution.py:70
  47.1 191.4 %all-reduce.7.cloned.1.call-start = ((), (), s32[]{:S(2)}) async-start(), calls=%async_computation.1 | async-start | bytes 393216 | tf_op jit(solution)/shard_map/psum | solution.py:93
  85.9 154.0 %copy-start.1 = (s32[32,96]{1,0:T(8,128)S(1)}, s32[32,96]{1,0:T(8,128)}, u32[]{:S(2)}) copy-start(s32[32,96]{1,0:T(8,128)} %param.15) | copy-start | bytes 36868
  239.4 42.6 %copy-start.2 = (f32[32,96]{1,0:T(8,128)}, f32[32,96]{1,0:T(8,128)S(1)}, u32[]{:S(2)}) copy-start(f32[32,96]{1,0:T(8,128)S(1)} %maximum_divide_fusion) | copy-start | bytes 36868
Sparse Core Ops, SparseCore 0:
  47.2 37.6 all-reduce.4
  184.9 53.6 all-reduce.6
